TPU v7x, 64 devices: a 2x2x8 block of a 4x4x8 slice. The times are simulated.
64 devices in a mesh: dp: 4 (over x, y), ep: 16 (over z, core).
Axes of the slice: x: 2, y: 2, z: 8, core: 2. Of those that a mesh axis runs over, the one named last changes fastest.
The devices are a block of a 4x4x8 slice.
Arguments:
- hidden: bfloat16 [16384, 2048], P(('dp', 'ep')), parts along dimension 0
- norm_gain: float32 [2048], replicated
- router_w: bfloat16 [2048, 64], replicated
- topk_idx: int32 [16384, 6], P(('dp', 'ep')), parts along dimension 0
- w_gate: bfloat16 [64, 2048, 1408], P('ep')
- w_up: bfloat16 [64, 2048, 1408], P('ep')
- w_down: bfloat16 [64, 1408, 2048], P('ep')
- shared_gate: bfloat16 [2048, 2816], replicated
- shared_up: bfloat16 [2048, 2816], replicated
- shared_down: bfloat16 [2816, 2048], replicated
Outputs:
- output: bfloat16 [16384, 2048], P(('dp', 'ep')), parts along dimension 0
There are 4 independent parts. A program takes and returns all parts, laid end to end along the dimension named above; an argument that names none is the same for every part.
All inputs are finite; a program needn't handle non-finite values.
Results may differ from a plain program's by a relative error of at most 0.00127.
Values are sent between devices in bfloat16 or wider.
A program may use at most 768 MiB of HBM per device.

v0:
```python
import functools

import jax
import jax.numpy as jnp
from jax import lax
from jax.experimental import pallas as pl
from jax.experimental.pallas import tpu as pltpu
from jax.sharding import PartitionSpec as P

NORM_EPS = 1e-6
CORES = 2
VMEM_LIMIT = 67043328
F32 = jnp.float32
BF16 = jnp.bfloat16


def slots_of(side, first_expert, local_count, before):
    ids, weights = side[0:8], side[8:16]
    chosen, picked = [], []
    for e in range(8):
        hit = ids == (first_expert + e).astype(F32)
        chosen.append(jnp.sum(jnp.where(hit, 1.0, 0.0), axis=0, keepdims=True))
        picked.append(jnp.sum(jnp.where(hit, weights, 0.0), axis=0, keepdims=True))
    chosen = jnp.concatenate(chosen, axis=0)
    rank = jnp.dot(chosen.astype(BF16), before, preferred_element_type=F32)
    slot = jnp.where(chosen > 0.5, rank, -1000.0)
    return [slot[e:e + 1] for e in range(local_count)], picked[:local_count]


def place_of(group_size):
    chips = group_size // CORES
    me = lax.axis_index('ep')
    chip, core = me // CORES, me % CORES
    right = (chip + 1) % chips * CORES + core
    left = (chip + chips - 1) % chips * CORES + core
    return me, chip, core, right, left, chip * CORES + (1 - core)


def enter(neighbours):
    barrier = pltpu.get_barrier_semaphore()
    for device in neighbours:
        pl.semaphore_signal(barrier, inc=1, device_id={'ep': device}, device_id_type=pl.DeviceIdType.MESH)
    pl.semaphore_wait(barrier, len(neighbours))


def remote(src, dst, send_sem, recv_sem, device):
    return pltpu.make_async_remote_copy(src_ref=src, dst_ref=dst, send_sem=send_sem, recv_sem=recv_sem,
                                        device_id={'ep': device}, device_id_type=pl.DeviceIdType.MESH)


def gather_kernel(group_size, capacity, slots, hidden_hbm, gain_ref, router_ref, idx_ref, before_ref,
                  sgate, sup, sdown, wgate, wup, wdown,
                  out_hbm, head_hbm, side_out, shared_ref,
                  rows, sides, x_ref, pick, gate_buf, up_buf, down_buf,
                  ring_s, ring_r, part_s, part_r, tring_s, tring_r, tpart_s, tpart_r, own_s, own_r,
                  head_s, head_r, load_sem, w_sem, out_sem):
    me, _, core, right, left, partner = place_of(group_size)
    local_count, hidden_size, ff = wgate.shape
    tokens = hidden_hbm.shape[0]
    half = tokens // 2
    half_cols = hidden_size // 2
    last = group_size // CORES - 1
    mine = pl.multiple_of(core * tokens, tokens)
    other = pl.multiple_of((1 - core) * tokens, tokens)

    def order(way, n):
        return min(2 * n + 1 + way, last)

    def piece(way, i, base):
        r = i % 2 if way == 0 else 1 - i % 2
        return rows.at[order(way, i // 2), pl.ds(pl.multiple_of(base + r * half, half), half)]

    def ring(way, i):
        n = i // 2
        r = i % 2 if way == 0 else 1 - i % 2
        src = 0 if n == 0 else order(way, n - 1)
        return remote(rows.at[src, pl.ds(pl.multiple_of(mine + r * half, half), half)], piece(way, i, mine),
                      ring_s.at[way, i], ring_r.at[way, i], right if way == 0 else left)

    def part(way, i, base):
        return remote(piece(way, i, base), piece(way, i, base), part_s.at[way, i], part_r.at[way, i], partner)

    def tring(way, n):
        src = 0 if n == 0 else 2 * (n - 1) + 1 + way
        return remote(sides.at[src, core], sides.at[2 * n + 1 + way, core],
                      tring_s.at[way, n], tring_r.at[way, n], right if way == 0 else left)

    def tpart(way, n, who):
        place = sides.at[2 * n + 1 + way, who]
        return remote(place, place, tpart_s.at[way, n], tpart_r.at[way, n], partner)

    def own_part(base):
        place = rows.at[0, pl.ds(base, tokens)]
        return remote(place, place, own_s.at[0], own_r.at[0], partner)

    def own_tpart(who):
        place = sides.at[0, who]
        return remote(place, place, own_s.at[1], own_r.at[1], partner)

    sends = 7

    def send(i):
        for way in range(2):
            ring(way, i).start()
            if i % 2 == 0 and i > 0:
                tring(way, i // 2).start()

    def service(i):
        for way in range(2):
            ring(way, i).wait_recv()
            if i % 2 == 0:
                tring(way, i // 2).wait_recv()
        if i + 2 < sends:
            send(i + 2)
        for way in range(2):
            part(way, i, mine).start()
            if i % 2 == 0:
                tpart(way, i // 2, core).start()

    def partner_arrived(i):
        for way in range(2):
            part(way, i, other).wait_recv()
            if i % 2 == 0:
                tpart(way, i // 2, 1 - core).wait_recv()

    def head(way, step, e):
        chip_row, cols = (((2, 0), (1, 1)), ((2, 1), (0, 0)))[way][step]
        return remote(x_ref.at[e, chip_row, :, cols * half_cols:(cols + 1) * half_cols], head_hbm.at[way, step, e],
                      head_s.at[way, step, e], head_r.at[way, step, e], right if way == 0 else left)

    load_rows = pltpu.make_async_copy(hidden_hbm, rows.at[0, pl.ds(mine, tokens)], load_sem.at[0])
    load_rows.start()

    def normalise():
        block = 32

        def one(i, carry):
            place = pl.ds(pl.multiple_of(mine + i * block, block), block)
            x = rows[0, place, :].astype(F32)
            inv_rms = lax.rsqrt(jnp.mean(x * x, axis=-1, keepdims=True) + NORM_EPS)
            rows[0, place, :] = (x * inv_rms * gain_ref[...]).astype(BF16)
            return carry
        lax.fori_loop(0, tokens // block, one, 0)

    def route():
        x = rows[0, pl.ds(mine, tokens), :]
        logits = lax.dot_general(router_ref[...], x, (((1,), (1,)), ((), ())), preferred_element_type=F32)
        top = jnp.exp(logits - jnp.max(logits, axis=0, keepdims=True))
        probs = top / jnp.sum(top, axis=0, keepdims=True)
        experts_id = lax.broadcasted_iota(jnp.int32, probs.shape, 0)
        sides[0, core] = jnp.full((16, tokens), -1.0, F32)
        for j in range(idx_ref.shape[0]):
            idx = idx_ref[j:j + 1, :]
            sides[0, core, j:j + 1, :] = idx.astype(F32)
            sides[0, core, 8 + j:9 + j, :] = jnp.sum(jnp.where(experts_id == idx, probs, 0.0), axis=0, keepdims=True)

    def gate_copies(slot, gate, up):
        return (pltpu.make_async_copy(gate, gate_buf.at[slot], w_sem.at[slot]),
                pltpu.make_async_copy(up, up_buf.at[slot], w_sem.at[2 + slot]))

    def start_gate(slot, gate, up):
        for copy in gate_copies(slot, gate, up):
            copy.start()

    def down_copy(down):
        return pltpu.make_async_copy(down, down_buf, w_sem.at[4])

    def shared_cols(ref, i):
        return ref.at[:, pl.ds(pl.multiple_of(i * ff, 128), ff)]

    start_gate(0, shared_cols(sgate, 0), shared_cols(sup, 0))
    enter((right, left, partner))
    load_rows.wait()
    normalise()
    send(0)
    send(1)
    own_part(mine).start()
    route()
    for way in range(2):
        tring(way, 0).start()
    own_tpart(core).start()

    def activate(x, slot):
        for copy in gate_copies(slot, wgate.at[0], wup.at[0]):
            copy.wait()
        gate_out = jnp.dot(x, gate_buf[slot], preferred_element_type=F32)
        up_out = jnp.dot(x, up_buf[slot], preferred_element_type=F32)
        return (jax.nn.silu(gate_out) * up_out).astype(BF16)

    def project(act):
        down_copy(wdown.at[0]).wait()
        return jnp.dot(act, down_buf[...], preferred_element_type=F32)

    shared_parts = sgate.shape[1] // ff

    def shared(i, carry):
        slot = i % 2
        down_copy(sdown.at[pl.ds(pl.multiple_of(i * ff, 128), ff)]).start()

        @pl.when(i < shared_parts - 1)
        def _():
            start_gate(1 - slot, shared_cols(sgate, i + 1), shared_cols(sup, i + 1))

        @pl.when(i == shared_parts - 1)
        def _():
            start_gate(1 - slot, wgate.at[0], wup.at[0])
        shared_ref[...] += project(activate(rows[0, pl.ds(mine, tokens), :], slot))
        return carry

    shared_ref[...] = jnp.zeros_like(shared_ref)
    lax.fori_loop(0, shared_parts, shared, 0)

    def dispatch(base, start, count):
        def one(ch, carry):
            for cc in range(CORES):
                slot, _ = slots_of(sides[ch, cc], me * local_count, local_count, before_ref[...])
                row_id = lax.broadcasted_iota(jnp.int32, (slots, tokens), 0).astype(F32)
                for e in range(local_count):
                    hit = row_id == slot[e] + float(capacity * cc)
                    pick[e * slots:(e + 1) * slots, cc * tokens:(cc + 1) * tokens] = jnp.where(hit, 1.0, 0.0).astype(BF16)
            step = min(512, hidden_size)
            for n in range(0, hidden_size, step):
                got = jnp.dot(pick[...], rows[ch, :, n:n + step], preferred_element_type=F32).astype(BF16)
                for e in range(local_count):
                    x_ref[e, ch - base, :, n:n + step] = got[e * slots:(e + 1) * slots]
            return carry
        lax.fori_loop(start, start + count, one, 0)

    def stage_copy(e, first, count):
        return pltpu.make_async_copy(x_ref.at[e, 0:count], out_hbm.at[e, pl.ds(first, count)], out_sem.at[e])

    def experts(first, count, middle):
        final = middle is None

        def one(e, carry):
            slot = e % 2
            if middle is not None:
                @pl.when(e == local_count // 2)
                def _():
                    service(middle)
            down_copy(wdown.at[e]).start()
            following = (e + 1) % local_count
            if final:
                @pl.when(e < local_count - 1)
                def _():
                    start_gate(1 - slot, wgate.at[following], wup.at[following])
            else:
                start_gate(1 - slot, wgate.at[following], wup.at[following])
            x = x_ref[e, 0:count].reshape(count * slots, hidden_size)
            out = project(activate(x, slot)).astype(BF16)
            x_ref[e, 0:count] = out.reshape(count, slots, hidden_size)
            if final:
                for step in range(2):
                    for way in range(2):
                        head(way, step, e).start()
            stage_copy(e, first, count).start()
            return carry
        lax.fori_loop(0, local_count, one, 0)

    def finish(first, count):
        for e in range(local_count):
            stage_copy(e, first, count).wait()

    service(0)
    own_part(other).wait_recv()
    own_tpart(1 - core).wait_recv()
    dispatch(0, 0, 1)
    service(1)
    partner_arrived(0)
    partner_arrived(1)
    dispatch(0, 1, 2)
    experts(0, 3, 2)
    finish(0, 3)
    service(3)
    partner_arrived(2)
    partner_arrived(3)
    dispatch(3, 3, 2)
    experts(3, 2, 4)
    finish(3, 2)
    service(5)
    partner_arrived(4)
    partner_arrived(5)
    dispatch(5, 5, 2)
    service(6)
    partner_arrived(6)
    dispatch(5, 7, 1)
    experts(5, 3, None)
    finish(5, 3)
    side_out[...] = sides[0:group_size // CORES]
    for way in range(2):
        for i in range(sends):
            ring(way, i).wait_send()
            part(way, i, mine).wait_send()
            if i % 2 == 0:
                tring(way, i // 2).wait_send()
                tpart(way, i // 2, core).wait_send()
    own_part(mine).wait_send()
    own_tpart(core).wait_send()
    for step in range(2):
        for way in range(2):
            for e in range(local_count):
                head(way, step, e).wait_recv()
                head(way, step, e).wait_send()


def scatter_kernel(group_size, capacity, rows_hbm, head_hbm, side_ref, before_ref, hidden_ref, shared_ref, out_ref,
                   rows, heads, acc, part_in, ring_in, load_sem, head_sem, ring_s, ring_r, part_s, part_r):
    me, _, core, right, left, partner = place_of(group_size)
    local_count, chips, _, hidden_size = rows.shape
    tokens = hidden_ref.shape[0]
    half = hidden_size // 2
    last = chips - 1
    steps = 5

    def load(ch):
        return pltpu.make_async_copy(rows_hbm.at[:, ch], rows.at[:, ch], load_sem.at[ch])

    def load_head(way, i):
        return pltpu.make_async_copy(head_hbm.at[way, i], heads.at[way, i], head_sem.at[way, i])

    for i in range(2):
        for way in range(2):
            load_head(way, i).start()
            load((last - 1, last - 2, 4, 3)[2 * i + way]).start()
    for ch in (2, 1, 0):
        load(ch).start()

    def ring(way, i):
        return remote(acc.at[0, way, i % 2], ring_in.at[way, i], ring_s.at[way, i], ring_r.at[way, i],
                      right if way == 0 else left)

    def part(way, i):
        return remote(acc.at[1, way, i % 2], part_in.at[way, i], part_s.at[way, i], part_r.at[way, i], partner)

    def mix_of(ch, cc, device):
        slot, weight = slots_of(side_ref[ch, cc], device * local_count, local_count, before_ref[...])
        row_id = lax.broadcasted_iota(jnp.int32, (WINDOW, tokens), 0).astype(F32)
        shift = (cc * (capacity - 32)).astype(F32)
        return [jnp.where(row_id == slot[e] + shift, weight[e], 0.0) for e in range(local_count)]

    def unit(ch, cc, h, way, i):
        start = pl.multiple_of(cc * 32, 32)
        col = pl.multiple_of(h * half, half)
        mix = mix_of(ch, cc, me)
        picked = [rows[e, ch, pl.ds(start, WINDOW), pl.ds(col, half)] for e in range(local_count)]
        if i < 2:
            mix += mix_of(ch, cc, left + way * (right - left))
            picked += [heads[way, i, e, pl.ds(start, WINDOW), :] for e in range(local_count)]
        mix = jnp.concatenate(mix, axis=0)
        picked = jnp.concatenate(picked, axis=0)
        high = mix.astype(BF16)
        rest = mix - high.astype(F32)
        mid = rest.astype(BF16)
        low = (rest - mid.astype(F32)).astype(BF16)
        total = jnp.dot(high.T, picked, preferred_element_type=F32)
        total += jnp.dot(mid.T, picked, preferred_element_type=F32)
        return total + jnp.dot(low.T, picked, preferred_element_type=F32)

    def units(i, chans, halves):
        def one(step, carry):
            who, way = 1 - step // 2, step % 2
            ch = chans[0] + way * (chans[1] - chans[0])
            h = halves[0] + way * (halves[1] - halves[0])
            cc = core + who - 2 * core * who
            acc[who, way, i % 2] = unit(ch, cc, h, way, i)

            @pl.when(step < 2)
            def _():
                part(way, i).start()
            return carry
        lax.fori_loop(0, 4, one, 0)

    enter((right, left, partner))
    loaded = set()

    def ensure(ch):
        if ch not in loaded:
            loaded.add(ch)
            load(ch).wait()

    for i in range(steps):
        k = 3 - (i + 1) // 2
        chans = (2 * k, 2 * k - 1)
        for ch in chans:
            ensure(ch)
        for way in range(2):
            if i < 2:
                load_head(way, i).wait()
            else:
                ring(way, i - 2).wait_send()
                part(way, i - 2).wait_send()
        units(i, chans, (i % 2, 1 - i % 2))
        for way in range(2):
            part(way, i).wait_recv()
            if i >= 2:
                ring(way, i - 2).wait_recv()
                acc[0, way, i % 2] = acc[0, way, i % 2] + part_in[way, i] + ring_in[way, i - 2]
            else:
                acc[0, way, i % 2] = acc[0, way, i % 2] + part_in[way, i]
            ring(way, i).start()
    ensure(0)
    for way in range(2):
        ring(way, steps - 2).wait_send()
        part(way, steps - 2).wait_send()
    units(steps, (0, 0), (0, 1))
    for h in range(2):
        part(h, steps).wait_recv()
        ring(1 - h, steps - 2).wait_recv()
        cols = slice(h * half, (h + 1) * half)
        acc[0, h, steps % 2] = (acc[0, h, steps % 2] + part_in[h, steps] + ring_in[1 - h, steps - 2]
                                + shared_ref[:, cols] + hidden_ref[:, cols].astype(F32))
    for h in range(2):
        ring(h, steps - 1).wait_recv()
        cols = slice(h * half, (h + 1) * half)
        out_ref[:, cols] = (acc[0, h, steps % 2] + ring_in[h, steps - 1]).astype(BF16)
    for way in range(2):
        ring(way, steps - 1).wait_send()
        part(way, steps - 1).wait_send()
        part(way, steps).wait_send()


WINDOW = 48


def solution(mesh):
    group_size = mesh.shape['ep']
    chips = group_size // CORES

    def local_step(hidden, norm_gain, router_w, topk_idx, w_gate, w_up, w_down, shared_gate, shared_up, shared_down):
        tokens, hidden_size = hidden.shape
        num_experts = router_w.shape[1]
        local_count, _, ff = w_gate.shape
        capacity = 3 * tokens * topk_idx.shape[1] // (2 * num_experts)
        slots = (CORES * capacity + 15) // 16 * 16
        before = jnp.triu(jnp.ones((tokens, tokens), BF16), 1)
        hbm = pl.BlockSpec(memory_space=pl.ANY)
        vmem = pl.BlockSpec(memory_space=pltpu.VMEM)
        dma = pltpu.SemaphoreType.DMA
        expert_out, heads, sides, shared_out = pl.pallas_call(
            functools.partial(gather_kernel, group_size, capacity, slots),
            in_specs=[hbm, vmem, vmem, vmem, vmem] + [hbm] * 6,
            out_specs=(hbm, hbm, vmem, vmem),
            out_shape=(jax.ShapeDtypeStruct((local_count, chips, slots, hidden_size), BF16),
                       jax.ShapeDtypeStruct((2, 2, local_count, slots, hidden_size // 2), BF16),
                       jax.ShapeDtypeStruct((chips, CORES, 16, tokens), F32),
                       jax.ShapeDtypeStruct((tokens, hidden_size), F32)),
            scratch_shapes=[
                pltpu.VMEM((chips, CORES * tokens, hidden_size), BF16),
                pltpu.VMEM((chips + 1, CORES, 16, tokens), F32),
                pltpu.VMEM((local_count, 3, slots, hidden_size), BF16),
                pltpu.VMEM((local_count * slots, CORES * tokens), BF16),
                pltpu.VMEM((2, hidden_size, ff), BF16),
                pltpu.VMEM((2, hidden_size, ff), BF16),
                pltpu.VMEM((ff, hidden_size), BF16),
                dma((2, 7)), dma((2, 7)), dma((2, 7)), dma((2, 7)),
                dma((2, 4)), dma((2, 4)), dma((2, 4)), dma((2, 4)),
                dma((2,)), dma((2,)), dma((2, 2, local_count)), dma((2, 2, local_count)),
                dma((1,)), dma((5,)), dma((local_count,)),
            ],
            compiler_params=pltpu.CompilerParams(collective_id=0, has_side_effects=True, vmem_limit_bytes=VMEM_LIMIT),
            name='gather_experts',
        )(hidden, norm_gain[None, :], router_w.T, topk_idx.T, before, shared_gate, shared_up, shared_down, w_gate, w_up, w_down)
        return pl.pallas_call(
            functools.partial(scatter_kernel, group_size, capacity),
            in_specs=[hbm, hbm, vmem, vmem, vmem, vmem],
            out_specs=vmem,
            out_shape=jax.ShapeDtypeStruct((tokens, hidden_size), BF16),
            scratch_shapes=[
                pltpu.VMEM((local_count, chips, slots, hidden_size), BF16),
                pltpu.VMEM((2, 2, local_count, slots, hidden_size // 2), BF16),
                pltpu.VMEM((2, 2, 2, tokens, hidden_size // 2), F32),
                pltpu.VMEM((2, 6, tokens, hidden_size // 2), F32),
                pltpu.VMEM((2, 5, tokens, hidden_size // 2), F32),
                dma((chips,)), dma((2, 2)), dma((2, 5)), dma((2, 5)), dma((2, 6)), dma((2, 6)),
            ],
            compiler_params=pltpu.CompilerParams(collective_id=1, has_side_effects=True, vmem_limit_bytes=VMEM_LIMIT),
            name='combine_scatter',
        )(expert_out, heads, sides, before, hidden, shared_out)

    token_spec = P(('dp', 'ep'), None)
    expert_spec = P('ep', None, None)
    return jax.shard_map(
        local_step,
        mesh=mesh,
        in_specs=(token_spec, P(None), P(None, None), token_spec, expert_spec, expert_spec, expert_spec,
                  P(None, None), P(None, None), P(None, None)),
        out_specs=token_spec,
        check_vma=False,
    )
```

profile of v0, /device:TPU:21, one launch (start us, length us, event | category | flops | bytes accessed | tf_op | source)
XLA Modules:
  0.0 265.4 jit_solution(14491618130675370217)
XLA Ops:
  0.0 0.7 fusion.before_ref
  0.7 137.3 %gather_experts.1 = (bf16[4,8,80,2048]{3,2,1,0:T(8,128)(2,1)}, bf16[2,2,4,80,1024]{4,3,2,1,0:T(8,128)(2,1)}, f32[8,2,16,256]{3,2,1,0:T(8,128)}, f32[256,2048]{1,0:T(8,128)}) custom-call(bf16[256,2048]{1,0:T(8,128)(2,1)} %hidden_ref.1, f32[1,2048]{1,0:T(1,128)} %bitcast.4, bf16[64,2048]{1,0:T(8,128)(2,1)} %bitcast.3, s32[6,256]{1,0:T(8,128)} %bitcast.5, ...), custom_call_target="tpu_custom_call" | custom-call | tf_op jit(solution)/shard_map/gather_experts/pallas_call | solution.py:439
  138.0 125.0 %combine_scatter.1 = bf16[256,2048]{1,0:T(8,128)(2,1)} custom-call(bf16[4,8,80,2048]{3,2,1,0:T(8,128)(2,1)} %get-tuple-element.9.rows_hbm, bf16[2,2,4,80,1024]{4,3,2,1,0:T(8,128)(2,1)} %get-tuple-element.10.head_hbm, f32[8,2,16,256]{3,2,1,0:T(8,128)} %get-tuple-element.11.side_ref, bf16[256,256]{1,0:T(8,128)(2,1)} %fusion.before_ref, ...), custom_call_target="tpu_custom_call" | custom-call | tf_op jit(solution)/shard_map/combine_scatter/pallas_call | solution.py:463
  263.0 2.3 copy.12
where the time goes:
time: 265 us
  Pallas kernels  262 us (99%)
    pallas_call x1, Pallas kernels, local_step(): pl.pallas_call(functools.partial(gather_kernel, group_size, capacity, slo...  137 us
    pallas_call x1, Pallas kernels, local_step(): pl.pallas_call(functools.partial(scatter_kernel, group_size, capacity), i...  125 us

commit v1 on v0

--- a/solution.py
+++ b/solution.py
@@ -50,10 +50,10 @@
 
 def gather_kernel(group_size, capacity, slots, hidden_hbm, gain_ref, router_ref, idx_ref, before_ref,
                   sgate, sup, sdown, wgate, wup, wdown,
-                  out_hbm, head_hbm, side_out, shared_ref,
+                  out_hbm, peer_hbm, head_hbm, side_out, shared_ref,
                   rows, sides, x_ref, pick, gate_buf, up_buf, down_buf,
                   ring_s, ring_r, part_s, part_r, tring_s, tring_r, tpart_s, tpart_r, own_s, own_r,
-                  head_s, head_r, load_sem, w_sem, out_sem):
+                  head_s, head_r, peer_s, peer_r, load_sem, w_sem, out_sem):
     me, _, core, right, left, partner = place_of(group_size)
     local_count, hidden_size, ff = wgate.shape
     tokens = hidden_hbm.shape[0]
@@ -123,10 +123,21 @@
             if i % 2 == 0:
                 tpart(way, i // 2, 1 - core).wait_recv()
 
-    def head(way, step, e):
+    beside = (right - core, left - core)
+
+    def head(way, step, e, cc, source):
         chip_row, cols = (((2, 0), (1, 1)), ((2, 1), (0, 0)))[way][step]
-        return remote(x_ref.at[e, chip_row, :, cols * half_cols:(cols + 1) * half_cols], head_hbm.at[way, step, e],
-                      head_s.at[way, step, e], head_r.at[way, step, e], right if way == 0 else left)
+        return remote(x_ref.at[e, chip_row, pl.ds(cc * HEAD_START, HEAD_ROWS), cols * half_cols:(cols + 1) * half_cols],
+                      head_hbm.at[way, step, source, e], head_s.at[way, step, e, cc], head_r.at[way, step, e, source],
+                      beside[way] + cc)
+
+    def send_heads(step, e):
+        for way in range(2):
+            for cc in range(CORES):
+                head(way, step, e, cc, core).start()
+
+    def peer(turn, first, count, e):
+        return remote(x_ref.at[e, 0:count], peer_hbm.at[e, pl.ds(first, count)], peer_s.at[turn, e], peer_r.at[turn, e], partner)
 
     load_rows = pltpu.make_async_copy(hidden_hbm, rows.at[0, pl.ds(mine, tokens)], load_sem.at[0])
     load_rows.start()
@@ -169,7 +180,7 @@
         return ref.at[:, pl.ds(pl.multiple_of(i * ff, 128), ff)]
 
     start_gate(0, shared_cols(sgate, 0), shared_cols(sup, 0))
-    enter((right, left, partner))
+    enter([device + cc for device in beside for cc in range(CORES)] + [partner])
     load_rows.wait()
     normalise()
     send(0)
@@ -180,15 +191,17 @@
         tring(way, 0).start()
     own_tpart(core).start()
 
-    def activate(x, slot):
-        for copy in gate_copies(slot, wgate.at[0], wup.at[0]):
-            copy.wait()
+    def activate(x, slot, fresh=True):
+        if fresh:
+            for copy in gate_copies(slot, wgate.at[0], wup.at[0]):
+                copy.wait()
         gate_out = jnp.dot(x, gate_buf[slot], preferred_element_type=F32)
         up_out = jnp.dot(x, up_buf[slot], preferred_element_type=F32)
         return (jax.nn.silu(gate_out) * up_out).astype(BF16)
 
-    def project(act):
-        down_copy(wdown.at[0]).wait()
+    def project(act, fresh=True):
+        if fresh:
+            down_copy(wdown.at[0]).wait()
         return jnp.dot(act, down_buf[...], preferred_element_type=F32)
 
     shared_parts = sgate.shape[1] // ff
@@ -229,37 +242,60 @@
     def stage_copy(e, first, count):
         return pltpu.make_async_copy(x_ref.at[e, 0:count], out_hbm.at[e, pl.ds(first, count)], out_sem.at[e])
 
-    def experts(first, count, middle):
-        final = middle is None
+    def start_next(e, slot):
+        down_copy(wdown.at[e]).start()
+        following = (e + 1) % local_count
+        start_gate(1 - slot, wgate.at[following], wup.at[following])
+
+    def mlp(e, slot, begin, count, fresh):
+        x = x_ref[e, begin:begin + count].reshape(count * slots, hidden_size)
+        out = project(activate(x, slot, fresh), fresh).astype(BF16)
+        x_ref[e, begin:begin + count] = out.reshape(count, slots, hidden_size)
+
+    def put(turn, first, count, e):
+        stage_copy(e, first, count).start()
+        peer(turn, first, count, e).start()
+
+    def experts(turn, first, count, middle):
+        def one(e, carry):
+            @pl.when(e == local_count // 2)
+            def _():
+                service(middle)
+            start_next(e, e % 2)
+            mlp(e, e % 2, 0, count, True)
+            put(turn, first, count, e)
+            return carry
+        lax.fori_loop(0, local_count, one, 0)
+
+    def last_experts(turn, first, count):
+        start_next(0, 0)
+        mlp(0, 0, 0, count - 1, True)
+        send_heads(1, 0)
+        service(6)
+        partner_arrived(6)
+        dispatch(first, first + count - 1, 1)
+        mlp(0, 0, count - 1, 1, False)
+        send_heads(0, 0)
+        put(turn, first, count, 0)
 
         def one(e, carry):
             slot = e % 2
-            if middle is not None:
-                @pl.when(e == local_count // 2)
-                def _():
-                    service(middle)
             down_copy(wdown.at[e]).start()
-            following = (e + 1) % local_count
-            if final:
-                @pl.when(e < local_count - 1)
-                def _():
-                    start_gate(1 - slot, wgate.at[following], wup.at[following])
-            else:
-                start_gate(1 - slot, wgate.at[following], wup.at[following])
-            x = x_ref[e, 0:count].reshape(count * slots, hidden_size)
-            out = project(activate(x, slot)).astype(BF16)
-            x_ref[e, 0:count] = out.reshape(count, slots, hidden_size)
-            if final:
-                for step in range(2):
-                    for way in range(2):
-                        head(way, step, e).start()
-            stage_copy(e, first, count).start()
+
+            @pl.when(e < local_count - 1)
+            def _():
+                start_gate(1 - slot, wgate.at[e + 1], wup.at[e + 1])
+            mlp(e, slot, 0, count, True)
+            send_heads(1, e)
+            send_heads(0, e)
+            put(turn, first, count, e)
             return carry
-        lax.fori_loop(0, local_count, one, 0)
-
-    def finish(first, count):
+        lax.fori_loop(1, local_count, one, 0)
+
+    def finish(turn, first, count):
         for e in range(local_count):
             stage_copy(e, first, count).wait()
+            peer(turn, first, count, e).wait_send()
 
     service(0)
     own_part(other).wait_recv()
@@ -269,23 +305,20 @@
     partner_arrived(0)
     partner_arrived(1)
     dispatch(0, 1, 2)
-    experts(0, 3, 2)
-    finish(0, 3)
+    experts(0, 0, 3, 2)
+    finish(0, 0, 3)
     service(3)
     partner_arrived(2)
     partner_arrived(3)
     dispatch(3, 3, 2)
-    experts(3, 2, 4)
-    finish(3, 2)
+    experts(1, 3, 2, 4)
+    finish(1, 3, 2)
     service(5)
     partner_arrived(4)
     partner_arrived(5)
     dispatch(5, 5, 2)
-    service(6)
-    partner_arrived(6)
-    dispatch(5, 7, 1)
-    experts(5, 3, None)
-    finish(5, 3)
+    last_experts(2, 5, 3)
+    finish(2, 5, 3)
     side_out[...] = sides[0:group_size // CORES]
     for way in range(2):
         for i in range(sends):
@@ -296,56 +329,65 @@
                 tpart(way, i // 2, core).wait_send()
     own_part(mine).wait_send()
     own_tpart(core).wait_send()
-    for step in range(2):
-        for way in range(2):
-            for e in range(local_count):
-                head(way, step, e).wait_recv()
-                head(way, step, e).wait_send()
-
-
-def scatter_kernel(group_size, capacity, rows_hbm, head_hbm, side_ref, before_ref, hidden_ref, shared_ref, out_ref,
-                   rows, heads, acc, part_in, ring_in, load_sem, head_sem, ring_s, ring_r, part_s, part_r):
-    me, _, core, right, left, partner = place_of(group_size)
-    local_count, chips, _, hidden_size = rows.shape
+    for turn, (first, count) in enumerate(((0, 3), (3, 2), (5, 3))):
+        for e in range(local_count):
+            peer(turn, first, count, e).wait_recv()
+
+    def settle(e, carry):
+        for step in range(2):
+            for way in range(2):
+                for cc in range(CORES):
+                    head(way, step, e, cc, cc).wait_recv()
+                    head(way, step, e, cc, cc).wait_send()
+        return carry
+    lax.fori_loop(0, local_count, settle, 0)
+
+
+def scatter_kernel(group_size, capacity, rows_hbm, peer_hbm, head_hbm, side_ref, before_ref, hidden_ref, shared_ref, out_ref,
+                   rows, heads, acc, ring_in, load_sem, head_sem, ring_s, ring_r):
+    _, chip, core, right, left, _ = place_of(group_size)
+    _, local_count, chips, _, hidden_size = rows.shape
     tokens = hidden_ref.shape[0]
     half = hidden_size // 2
     last = chips - 1
     steps = 5
+    window = pl.ds(pl.multiple_of(core * HEAD_START, HEAD_START), WINDOW)
 
     def load(ch):
-        return pltpu.make_async_copy(rows_hbm.at[:, ch], rows.at[:, ch], load_sem.at[ch])
+        return (pltpu.make_async_copy(rows_hbm.at[:, ch, window], rows.at[core, :, ch], load_sem.at[0, ch]),
+                pltpu.make_async_copy(peer_hbm.at[:, ch, window], rows.at[1 - core, :, ch], load_sem.at[1, ch]))
 
     def load_head(way, i):
-        return pltpu.make_async_copy(head_hbm.at[way, i], heads.at[way, i], head_sem.at[way, i])
+        return pltpu.make_async_copy(head_hbm.at[way, i], heads.at[way, i, :, :, 0:HEAD_ROWS], head_sem.at[way, i])
 
     for i in range(2):
         for way in range(2):
             load_head(way, i).start()
-            load((last - 1, last - 2, 4, 3)[2 * i + way]).start()
+            for copy in load((last - 1, last - 2, 4, 3)[2 * i + way]):
+                copy.start()
     for ch in (2, 1, 0):
-        load(ch).start()
+        for copy in load(ch):
+            copy.start()
+    heads[:, :, :, :, HEAD_ROWS:WINDOW, :] = jnp.zeros((2, 2, CORES, local_count, WINDOW - HEAD_ROWS, half), BF16)
 
     def ring(way, i):
-        return remote(acc.at[0, way, i % 2], ring_in.at[way, i], ring_s.at[way, i], ring_r.at[way, i],
+        return remote(acc.at[way, i % 2], ring_in.at[way, i], ring_s.at[way, i], ring_r.at[way, i],
                       right if way == 0 else left)
 
-    def part(way, i):
-        return remote(acc.at[1, way, i % 2], part_in.at[way, i], part_s.at[way, i], part_r.at[way, i], partner)
-
-    def mix_of(ch, cc, device):
-        slot, weight = slots_of(side_ref[ch, cc], device * local_count, local_count, before_ref[...])
+    def mix_of(ch, from_chip):
+        count = CORES * local_count
+        slot, weight = slots_of(side_ref[ch, core], from_chip * count, count, before_ref[...])
         row_id = lax.broadcasted_iota(jnp.int32, (WINDOW, tokens), 0).astype(F32)
-        shift = (cc * (capacity - 32)).astype(F32)
-        return [jnp.where(row_id == slot[e] + shift, weight[e], 0.0) for e in range(local_count)]
-
-    def unit(ch, cc, h, way, i):
-        start = pl.multiple_of(cc * 32, 32)
+        shift = (core * (capacity - HEAD_START)).astype(F32)
+        return [jnp.where(row_id == slot[e] + shift, weight[e], 0.0) for e in range(count)]
+
+    def unit(ch, h, way, i):
         col = pl.multiple_of(h * half, half)
-        mix = mix_of(ch, cc, me)
-        picked = [rows[e, ch, pl.ds(start, WINDOW), pl.ds(col, half)] for e in range(local_count)]
+        mix = mix_of(ch, chip)
+        picked = [rows[cc, e, ch, :, pl.ds(col, half)] for cc in range(CORES) for e in range(local_count)]
         if i < 2:
-            mix += mix_of(ch, cc, left + way * (right - left))
-            picked += [heads[way, i, e, pl.ds(start, WINDOW), :] for e in range(local_count)]
+            mix += mix_of(ch, (left + way * (right - left)) // CORES)
+            picked += [heads[way, i, cc, e] for cc in range(CORES) for e in range(local_count)]
         mix = jnp.concatenate(mix, axis=0)
         picked = jnp.concatenate(picked, axis=0)
         high = mix.astype(BF16)
@@ -357,26 +399,21 @@
         return total + jnp.dot(low.T, picked, preferred_element_type=F32)
 
     def units(i, chans, halves):
-        def one(step, carry):
-            who, way = 1 - step // 2, step % 2
+        def one(way, carry):
             ch = chans[0] + way * (chans[1] - chans[0])
             h = halves[0] + way * (halves[1] - halves[0])
-            cc = core + who - 2 * core * who
-            acc[who, way, i % 2] = unit(ch, cc, h, way, i)
-
-            @pl.when(step < 2)
-            def _():
-                part(way, i).start()
+            acc[way, i % 2] = unit(ch, h, way, i)
             return carry
-        lax.fori_loop(0, 4, one, 0)
-
-    enter((right, left, partner))
+        lax.fori_loop(0, 2, one, 0)
+
+    enter((right, left))
     loaded = set()
 
     def ensure(ch):
         if ch not in loaded:
             loaded.add(ch)
-            load(ch).wait()
+            for copy in load(ch):
+                copy.wait()
 
     for i in range(steps):
         k = 3 - (i + 1) // 2
@@ -388,38 +425,32 @@
                 load_head(way, i).wait()
             else:
                 ring(way, i - 2).wait_send()
-                part(way, i - 2).wait_send()
         units(i, chans, (i % 2, 1 - i % 2))
         for way in range(2):
-            part(way, i).wait_recv()
             if i >= 2:
                 ring(way, i - 2).wait_recv()
-                acc[0, way, i % 2] = acc[0, way, i % 2] + part_in[way, i] + ring_in[way, i - 2]
-            else:
-                acc[0, way, i % 2] = acc[0, way, i % 2] + part_in[way, i]
+                acc[way, i % 2] = acc[way, i % 2] + ring_in[way, i - 2]
             ring(way, i).start()
     ensure(0)
     for way in range(2):
         ring(way, steps - 2).wait_send()
-        part(way, steps - 2).wait_send()
     units(steps, (0, 0), (0, 1))
     for h in range(2):
-        part(h, steps).wait_recv()
         ring(1 - h, steps - 2).wait_recv()
         cols = slice(h * half, (h + 1) * half)
-        acc[0, h, steps % 2] = (acc[0, h, steps % 2] + part_in[h, steps] + ring_in[1 - h, steps - 2]
-                                + shared_ref[:, cols] + hidden_ref[:, cols].astype(F32))
+        acc[h, steps % 2] = (acc[h, steps % 2] + ring_in[1 - h, steps - 2]
+                             + shared_ref[:, cols] + hidden_ref[:, cols].astype(F32))
     for h in range(2):
         ring(h, steps - 1).wait_recv()
         cols = slice(h * half, (h + 1) * half)
-        out_ref[:, cols] = (acc[0, h, steps % 2] + ring_in[h, steps - 1]).astype(BF16)
+        out_ref[:, cols] = (acc[h, steps % 2] + ring_in[h, steps - 1]).astype(BF16)
     for way in range(2):
         ring(way, steps - 1).wait_send()
-        part(way, steps - 1).wait_send()
-        part(way, steps).wait_send()
 
 
 WINDOW = 48
+HEAD_START = 32
+HEAD_ROWS = 40
 
 
 def solution(mesh):
@@ -436,12 +467,13 @@
         hbm = pl.BlockSpec(memory_space=pl.ANY)
         vmem = pl.BlockSpec(memory_space=pltpu.VMEM)
         dma = pltpu.SemaphoreType.DMA
-        expert_out, heads, sides, shared_out = pl.pallas_call(
+        expert_out, peer_out, heads, sides, shared_out = pl.pallas_call(
             functools.partial(gather_kernel, group_size, capacity, slots),
             in_specs=[hbm, vmem, vmem, vmem, vmem] + [hbm] * 6,
-            out_specs=(hbm, hbm, vmem, vmem),
+            out_specs=(hbm, hbm, hbm, vmem, vmem),
             out_shape=(jax.ShapeDtypeStruct((local_count, chips, slots, hidden_size), BF16),
-                       jax.ShapeDtypeStruct((2, 2, local_count, slots, hidden_size // 2), BF16),
+                       jax.ShapeDtypeStruct((local_count, chips, slots, hidden_size), BF16),
+                       jax.ShapeDtypeStruct((2, 2, CORES, local_count, HEAD_ROWS, hidden_size // 2), BF16),
                        jax.ShapeDtypeStruct((chips, CORES, 16, tokens), F32),
                        jax.ShapeDtypeStruct((tokens, hidden_size), F32)),
             scratch_shapes=[
@@ -454,7 +486,8 @@
                 pltpu.VMEM((ff, hidden_size), BF16),
                 dma((2, 7)), dma((2, 7)), dma((2, 7)), dma((2, 7)),
                 dma((2, 4)), dma((2, 4)), dma((2, 4)), dma((2, 4)),
-                dma((2,)), dma((2,)), dma((2, 2, local_count)), dma((2, 2, local_count)),
+                dma((2,)), dma((2,)), dma((2, 2, local_count, CORES)), dma((2, 2, local_count, CORES)),
+                dma((3, local_count)), dma((3, local_count)),
                 dma((1,)), dma((5,)), dma((local_count,)),
             ],
             compiler_params=pltpu.CompilerParams(collective_id=0, has_side_effects=True, vmem_limit_bytes=VMEM_LIMIT),
@@ -462,20 +495,19 @@
         )(hidden, norm_gain[None, :], router_w.T, topk_idx.T, before, shared_gate, shared_up, shared_down, w_gate, w_up, w_down)
         return pl.pallas_call(
             functools.partial(scatter_kernel, group_size, capacity),
-            in_specs=[hbm, hbm, vmem, vmem, vmem, vmem],
+            in_specs=[hbm, hbm, hbm, vmem, vmem, vmem, vmem],
             out_specs=vmem,
             out_shape=jax.ShapeDtypeStruct((tokens, hidden_size), BF16),
             scratch_shapes=[
-                pltpu.VMEM((local_count, chips, slots, hidden_size), BF16),
-                pltpu.VMEM((2, 2, local_count, slots, hidden_size // 2), BF16),
-                pltpu.VMEM((2, 2, 2, tokens, hidden_size // 2), F32),
-                pltpu.VMEM((2, 6, tokens, hidden_size // 2), F32),
+                pltpu.VMEM((CORES, local_count, chips, WINDOW, hidden_size), BF16),
+                pltpu.VMEM((2, 2, CORES, local_count, WINDOW, hidden_size // 2), BF16),
+                pltpu.VMEM((2, 2, tokens, hidden_size // 2), F32),
                 pltpu.VMEM((2, 5, tokens, hidden_size // 2), F32),
-                dma((chips,)), dma((2, 2)), dma((2, 5)), dma((2, 5)), dma((2, 6)), dma((2, 6)),
+                dma((CORES, chips)), dma((2, 2)), dma((2, 5)), dma((2, 5)),
             ],
             compiler_params=pltpu.CompilerParams(collective_id=1, has_side_effects=True, vmem_limit_bytes=VMEM_LIMIT),
             name='combine_scatter',
-        )(expert_out, heads, sides, before, hidden, shared_out)
+        )(expert_out, peer_out, heads, sides, before, hidden, shared_out)
 
     token_spec = P(('dp', 'ep'), None)
     expert_spec = P('ep', None, None)

time: 265 us -> 267 us (level)
  no operation moved by 1% of the time
where the time goes in v1:
time: 267 us
  Pallas kernels  264 us (99%)
    pallas_call x1, Pallas kernels, local_step(): pl.pallas_call(functools.partial(gather_kernel, group_size, capacity, slo...  138 us
    pallas_call x1, Pallas kernels, local_step(): pl.pallas_call(functools.partial(scatter_kernel, group_size, capacity), i...  126 us

profile of v1, /device:TPU:21, one launch (start us, length us, event | category | flops | bytes accessed | tf_op | source)
XLA Modules:
  0.0 267.3 jit_solution(9831803647194867090)
XLA Ops:
  0.0 0.7 fusion.before_ref
  0.7 138.2 %gather_experts.1 = (bf16[4,8,80,2048]{3,2,1,0:T(8,128)(2,1)}, bf16[4,8,80,2048]{3,2,1,0:T(8,128)(2,1)}, bf16[2,2,2,4,40,1024]{5,4,3,2,1,0:T(8,128)(2,1)}, f32[8,2,16,256]{3,2,1,0:T(8,128)}, f32[256,2048]{1,0:T(8,128)}) custom-call(bf16[256,2048]{1,0:T(8,128)(2,1)} %hidden_ref.1, f32[1,2048]{1,0:T(1,128)} %bitcast.4, bf16[64,2048]{1,0:T(8,128)(2,1)} %bitcast.3, ...), custom_call_target="tpu_custom_call" | custom-call | tf_op jit(solution)/shard_map/gather_experts/pallas_call | solution.py:470
  138.8 126.1 %combine_scatter.1 = bf16[256,2048]{1,0:T(8,128)(2,1)} custom-call(bf16[4,8,80,2048]{3,2,1,0:T(8,128)(2,1)} %get-tuple-element.10.rows_hbm, bf16[4,8,80,2048]{3,2,1,0:T(8,128)(2,1)} %get-tuple-element.11.peer_hbm, bf16[2,2,2,4,40,1024]{5,4,3,2,1,0:T(8,128)(2,1)} %get-tuple-element.12.head_hbm, f32[8,2,16,256]{3,2,1,0:T(8,128)} %get-tuple-element.13.side_ref, ...), custom_call_target="tpu_custom_call" | custom-call | tf_op jit(solution)/shard_map/combine_scatter/pallas_call | solution.py:496
  265.0 2.3 copy.12

commit v2 on v1

--- a/solution.py
+++ b/solution.py
@@ -36,11 +36,20 @@
     return me, chip, core, right, left, chip * CORES + (1 - core)
 
 
-def enter(neighbours):
-    barrier = pltpu.get_barrier_semaphore()
+def announce(neighbours):
     for device in neighbours:
-        pl.semaphore_signal(barrier, inc=1, device_id={'ep': device}, device_id_type=pl.DeviceIdType.MESH)
-    pl.semaphore_wait(barrier, len(neighbours))
+        pl.semaphore_signal(pltpu.get_barrier_semaphore(), inc=1, device_id={'ep': device},
+                            device_id_type=pl.DeviceIdType.MESH)
+
+
+def meet(neighbours):
+    pl.semaphore_wait(pltpu.get_barrier_semaphore(), len(neighbours))
+
+
+def fill_before(before):
+    row = lax.broadcasted_iota(jnp.int32, before.shape, 0)
+    col = lax.broadcasted_iota(jnp.int32, before.shape, 1)
+    before[...] = jnp.where(row < col, 1.0, 0.0).astype(BF16)
 
 
 def remote(src, dst, send_sem, recv_sem, device):
@@ -48,10 +57,10 @@
                                         device_id={'ep': device}, device_id_type=pl.DeviceIdType.MESH)
 
 
-def gather_kernel(group_size, capacity, slots, hidden_hbm, gain_ref, router_ref, idx_ref, before_ref,
+def gather_kernel(group_size, capacity, slots, hidden_hbm, gain_ref, router_ref, idx_ref,
                   sgate, sup, sdown, wgate, wup, wdown,
                   out_hbm, peer_hbm, head_hbm, side_out, shared_ref,
-                  rows, sides, x_ref, pick, gate_buf, up_buf, down_buf,
+                  before_ref, rows, sides, x_ref, pick, gate_buf, up_buf, down_buf,
                   ring_s, ring_r, part_s, part_r, tring_s, tring_r, tpart_s, tpart_r, own_s, own_r,
                   head_s, head_r, peer_s, peer_r, load_sem, w_sem, out_sem):
     me, _, core, right, left, partner = place_of(group_size)
@@ -179,10 +188,15 @@
     def shared_cols(ref, i):
         return ref.at[:, pl.ds(pl.multiple_of(i * ff, 128), ff)]
 
+    neighbours = [device + cc for device in beside for cc in range(CORES)] + [partner]
+    announce(neighbours)
     start_gate(0, shared_cols(sgate, 0), shared_cols(sup, 0))
-    enter([device + cc for device in beside for cc in range(CORES)] + [partner])
+    down_copy(sdown.at[0:ff]).start()
+    start_gate(1, shared_cols(sgate, 1), shared_cols(sup, 1))
+    fill_before(before_ref)
     load_rows.wait()
     normalise()
+    meet(neighbours)
     send(0)
     send(1)
     own_part(mine).start()
@@ -191,33 +205,38 @@
         tring(way, 0).start()
     own_tpart(core).start()
 
-    def activate(x, slot, fresh=True):
+    def swiglu(x, slot, fresh, next_gate, next_down):
         if fresh:
             for copy in gate_copies(slot, wgate.at[0], wup.at[0]):
                 copy.wait()
         gate_out = jnp.dot(x, gate_buf[slot], preferred_element_type=F32)
         up_out = jnp.dot(x, up_buf[slot], preferred_element_type=F32)
-        return (jax.nn.silu(gate_out) * up_out).astype(BF16)
-
-    def project(act, fresh=True):
+        act = (jax.nn.silu(gate_out) * up_out).astype(BF16)
+        next_gate()
         if fresh:
             down_copy(wdown.at[0]).wait()
-        return jnp.dot(act, down_buf[...], preferred_element_type=F32)
-
-    shared_parts = sgate.shape[1] // ff
+        out = jnp.dot(act, down_buf[...], preferred_element_type=F32)
+        next_down()
+        return out
+
+    def nothing():
+        pass
+
+    shared_parts = 2
 
     def shared(i, carry):
         slot = i % 2
-        down_copy(sdown.at[pl.ds(pl.multiple_of(i * ff, 128), ff)]).start()
-
-        @pl.when(i < shared_parts - 1)
-        def _():
-            start_gate(1 - slot, shared_cols(sgate, i + 1), shared_cols(sup, i + 1))
-
-        @pl.when(i == shared_parts - 1)
-        def _():
-            start_gate(1 - slot, wgate.at[0], wup.at[0])
-        shared_ref[...] += project(activate(rows[0, pl.ds(mine, tokens), :], slot))
+
+        def next_down():
+            @pl.when(i == 0)
+            def _():
+                down_copy(sdown.at[ff:2 * ff]).start()
+
+            @pl.when(i == 1)
+            def _():
+                down_copy(wdown.at[0]).start()
+        shared_ref[...] += swiglu(rows[0, pl.ds(mine, tokens), :], slot, True,
+                                  lambda: start_gate(slot, wgate.at[i], wup.at[i]), next_down)
         return carry
 
     shared_ref[...] = jnp.zeros_like(shared_ref)
@@ -242,15 +261,17 @@
     def stage_copy(e, first, count):
         return pltpu.make_async_copy(x_ref.at[e, 0:count], out_hbm.at[e, pl.ds(first, count)], out_sem.at[e])
 
-    def start_next(e, slot):
-        down_copy(wdown.at[e]).start()
-        following = (e + 1) % local_count
-        start_gate(1 - slot, wgate.at[following], wup.at[following])
-
-    def mlp(e, slot, begin, count, fresh):
+    def mlp(e, slot, begin, count, fresh, next_gate, next_down):
         x = x_ref[e, begin:begin + count].reshape(count * slots, hidden_size)
-        out = project(activate(x, slot, fresh), fresh).astype(BF16)
+        out = swiglu(x, slot, fresh, next_gate, next_down).astype(BF16)
         x_ref[e, begin:begin + count] = out.reshape(count, slots, hidden_size)
+
+    def gate_after(e, slot):
+        ahead = (e + 2) % local_count
+        start_gate(slot, wgate.at[ahead], wup.at[ahead])
+
+    def down_after(e):
+        down_copy(wdown.at[(e + 1) % local_count]).start()
 
     def put(turn, first, count, e):
         stage_copy(e, first, count).start()
@@ -261,31 +282,32 @@
             @pl.when(e == local_count // 2)
             def _():
                 service(middle)
-            start_next(e, e % 2)
-            mlp(e, e % 2, 0, count, True)
+            mlp(e, e % 2, 0, count, True, lambda: gate_after(e, e % 2), lambda: down_after(e))
             put(turn, first, count, e)
             return carry
         lax.fori_loop(0, local_count, one, 0)
 
     def last_experts(turn, first, count):
-        start_next(0, 0)
-        mlp(0, 0, 0, count - 1, True)
+        mlp(0, 0, 0, count - 1, True, nothing, nothing)
         send_heads(1, 0)
         service(6)
         partner_arrived(6)
         dispatch(first, first + count - 1, 1)
-        mlp(0, 0, count - 1, 1, False)
+        mlp(0, 0, count - 1, 1, False, lambda: gate_after(0, 0), lambda: down_after(0))
         send_heads(0, 0)
         put(turn, first, count, 0)
 
         def one(e, carry):
-            slot = e % 2
-            down_copy(wdown.at[e]).start()
-
-            @pl.when(e < local_count - 1)
-            def _():
-                start_gate(1 - slot, wgate.at[e + 1], wup.at[e + 1])
-            mlp(e, slot, 0, count, True)
+            def next_gate():
+                @pl.when(e < local_count - 2)
+                def _():
+                    gate_after(e, e % 2)
+
+            def next_down():
+                @pl.when(e < local_count - 1)
+                def _():
+                    down_after(e)
+            mlp(e, e % 2, 0, count, True, next_gate, next_down)
             send_heads(1, e)
             send_heads(0, e)
             put(turn, first, count, e)
@@ -343,8 +365,8 @@
     lax.fori_loop(0, local_count, settle, 0)
 
 
-def scatter_kernel(group_size, capacity, rows_hbm, peer_hbm, head_hbm, side_ref, before_ref, hidden_ref, shared_ref, out_ref,
-                   rows, heads, acc, ring_in, load_sem, head_sem, ring_s, ring_r):
+def scatter_kernel(group_size, capacity, rows_hbm, peer_hbm, head_hbm, side_ref, hidden_hbm, shared_hbm, out_ref,
+                   before_ref, hidden_ref, shared_ref, rows, heads, acc, ring_in, load_sem, head_sem, base_sem, ring_s, ring_r):
     _, chip, core, right, left, _ = place_of(group_size)
     _, local_count, chips, _, hidden_size = rows.shape
     tokens = hidden_ref.shape[0]
@@ -360,6 +382,8 @@
     def load_head(way, i):
         return pltpu.make_async_copy(head_hbm.at[way, i], heads.at[way, i, :, :, 0:HEAD_ROWS], head_sem.at[way, i])
 
+    neighbours = (right, left)
+    announce(neighbours)
     for i in range(2):
         for way in range(2):
             load_head(way, i).start()
@@ -368,6 +392,11 @@
     for ch in (2, 1, 0):
         for copy in load(ch):
             copy.start()
+    load_base = (pltpu.make_async_copy(hidden_hbm, hidden_ref, base_sem.at[0]),
+                 pltpu.make_async_copy(shared_hbm, shared_ref, base_sem.at[1]))
+    for copy in load_base:
+        copy.start()
+    fill_before(before_ref)
     heads[:, :, :, :, HEAD_ROWS:WINDOW, :] = jnp.zeros((2, 2, CORES, local_count, WINDOW - HEAD_ROWS, half), BF16)
 
     def ring(way, i):
@@ -406,7 +435,6 @@
             return carry
         lax.fori_loop(0, 2, one, 0)
 
-    enter((right, left))
     loaded = set()
 
     def ensure(ch):
@@ -426,6 +454,8 @@
             else:
                 ring(way, i - 2).wait_send()
         units(i, chans, (i % 2, 1 - i % 2))
+        if i == 0:
+            meet(neighbours)
         for way in range(2):
             if i >= 2:
                 ring(way, i - 2).wait_recv()
@@ -435,6 +465,8 @@
     for way in range(2):
         ring(way, steps - 2).wait_send()
     units(steps, (0, 0), (0, 1))
+    for copy in load_base:
+        copy.wait()
     for h in range(2):
         ring(1 - h, steps - 2).wait_recv()
         cols = slice(h * half, (h + 1) * half)
@@ -463,13 +495,12 @@
         local_count, _, ff = w_gate.shape
         capacity = 3 * tokens * topk_idx.shape[1] // (2 * num_experts)
         slots = (CORES * capacity + 15) // 16 * 16
-        before = jnp.triu(jnp.ones((tokens, tokens), BF16), 1)
         hbm = pl.BlockSpec(memory_space=pl.ANY)
         vmem = pl.BlockSpec(memory_space=pltpu.VMEM)
         dma = pltpu.SemaphoreType.DMA
         expert_out, peer_out, heads, sides, shared_out = pl.pallas_call(
             functools.partial(gather_kernel, group_size, capacity, slots),
-            in_specs=[hbm, vmem, vmem, vmem, vmem] + [hbm] * 6,
+            in_specs=[hbm, vmem, vmem, vmem] + [hbm] * 6,
             out_specs=(hbm, hbm, hbm, vmem, vmem),
             out_shape=(jax.ShapeDtypeStruct((local_count, chips, slots, hidden_size), BF16),
                        jax.ShapeDtypeStruct((local_count, chips, slots, hidden_size), BF16),
@@ -477,6 +508,7 @@
                        jax.ShapeDtypeStruct((chips, CORES, 16, tokens), F32),
                        jax.ShapeDtypeStruct((tokens, hidden_size), F32)),
             scratch_shapes=[
+                pltpu.VMEM((tokens, tokens), BF16),
                 pltpu.VMEM((chips, CORES * tokens, hidden_size), BF16),
                 pltpu.VMEM((chips + 1, CORES, 16, tokens), F32),
                 pltpu.VMEM((local_count, 3, slots, hidden_size), BF16),
@@ -492,22 +524,25 @@
             ],
             compiler_params=pltpu.CompilerParams(collective_id=0, has_side_effects=True, vmem_limit_bytes=VMEM_LIMIT),
             name='gather_experts',
-        )(hidden, norm_gain[None, :], router_w.T, topk_idx.T, before, shared_gate, shared_up, shared_down, w_gate, w_up, w_down)
+        )(hidden, norm_gain[None, :], router_w.T, topk_idx.T, shared_gate, shared_up, shared_down, w_gate, w_up, w_down)
         return pl.pallas_call(
             functools.partial(scatter_kernel, group_size, capacity),
-            in_specs=[hbm, hbm, hbm, vmem, vmem, vmem, vmem],
+            in_specs=[hbm, hbm, hbm, vmem, hbm, hbm],
             out_specs=vmem,
             out_shape=jax.ShapeDtypeStruct((tokens, hidden_size), BF16),
             scratch_shapes=[
+                pltpu.VMEM((tokens, tokens), BF16),
+                pltpu.VMEM((tokens, hidden_size), BF16),
+                pltpu.VMEM((tokens, hidden_size), F32),
                 pltpu.VMEM((CORES, local_count, chips, WINDOW, hidden_size), BF16),
                 pltpu.VMEM((2, 2, CORES, local_count, WINDOW, hidden_size // 2), BF16),
                 pltpu.VMEM((2, 2, tokens, hidden_size // 2), F32),
                 pltpu.VMEM((2, 5, tokens, hidden_size // 2), F32),
-                dma((CORES, chips)), dma((2, 2)), dma((2, 5)), dma((2, 5)),
+                dma((CORES, chips)), dma((2, 2)), dma((2,)), dma((2, 5)), dma((2, 5)),
             ],
             compiler_params=pltpu.CompilerParams(collective_id=1, has_side_effects=True, vmem_limit_bytes=VMEM_LIMIT),
             name='combine_scatter',
-        )(expert_out, peer_out, heads, sides, before, hidden, shared_out)
+        )(expert_out, peer_out, heads, sides, hidden, shared_out)
 
     token_spec = P(('dp', 'ep'), None)
     expert_spec = P('ep', None, None)

time: 267 us -> 262 us (0.981)
  Pallas kernels: 264 us -> 259 us
    pallas_call x1, Pallas kernels: 138 us -> 135 us  [local_step(): pl.pallas_call(functools.partial(gather_kernel, group_size, capacity, slo...]
where the time goes in v2:
time: 262 us
  Pallas kernels  259 us (99%)
    pallas_call x1, Pallas kernels, local_step(): pl.pallas_call(functools.partial(gather_kernel, group_size, capacity, slo...  135 us
    pallas_call x1, Pallas kernels, local_step(): pl.pallas_call(functools.partial(scatter_kernel, group_size, capacity), i...  125 us

profile of v2, /device:TPU:21, one launch (start us, length us, event | category | flops | bytes accessed | tf_op | source)
XLA Modules:
  0.0 261.6 jit_solution(1536243325232741250)
XLA Ops:
  0.0 134.8 %gather_experts.1 = (bf16[4,8,80,2048]{3,2,1,0:T(8,128)(2,1)}, bf16[4,8,80,2048]{3,2,1,0:T(8,128)(2,1)}, bf16[2,2,2,4,40,1024]{5,4,3,2,1,0:T(8,128)(2,1)}, f32[8,2,16,256]{3,2,1,0:T(8,128)}, f32[256,2048]{1,0:T(8,128)}) custom-call(bf16[256,2048]{1,0:T(8,128)(2,1)} %hidden_hbm.3, f32[1,2048]{1,0:T(1,128)} %bitcast.4, bf16[64,2048]{1,0:T(8,128)(2,1)} %bitcast.3, ...), custom_call_target="tpu_custom_call" | custom-call | tf_op jit(solution)/shard_map/gather_experts/pallas_call | solution.py:501
  134.8 124.5 %combine_scatter.1 = bf16[256,2048]{1,0:T(8,128)(2,1)} custom-call(bf16[4,8,80,2048]{3,2,1,0:T(8,128)(2,1)} %get-tuple-element.10.rows_hbm, bf16[4,8,80,2048]{3,2,1,0:T(8,128)(2,1)} %get-tuple-element.11.peer_hbm, bf16[2,2,2,4,40,1024]{5,4,3,2,1,0:T(8,128)(2,1)} %get-tuple-element.12.head_hbm, f32[8,2,16,256]{3,2,1,0:T(8,128)} %get-tuple-element.13.side_ref, ...), custom_call_target="tpu_custom_call" | custom-call | tf_op jit(solution)/shard_map/combine_scatter/pallas_call | solution.py:528
  259.3 2.3 copy.12

commit v3 on v2

--- a/solution.py
+++ b/solution.py
@@ -57,10 +57,10 @@
                                         device_id={'ep': device}, device_id_type=pl.DeviceIdType.MESH)
 
 
-def gather_kernel(group_size, capacity, slots, hidden_hbm, gain_ref, router_ref, idx_ref,
+def gather_kernel(group_size, capacity, slots, hidden_hbm, gain_hbm, router_hbm, idx_hbm,
                   sgate, sup, sdown, wgate, wup, wdown,
-                  out_hbm, peer_hbm, head_hbm, side_out, shared_ref,
-                  before_ref, rows, sides, x_ref, pick, gate_buf, up_buf, down_buf,
+                  out_hbm, peer_hbm, head_hbm, side_hbm, shared_hbm,
+                  gain_ref, router_ref, idx_ref, shared_ref, before_ref, rows, sides, x_ref, pick, gate_buf, up_buf, down_buf,
                   ring_s, ring_r, part_s, part_r, tring_s, tring_r, tpart_s, tpart_r, own_s, own_r,
                   head_s, head_r, peer_s, peer_r, load_sem, w_sem, out_sem):
     me, _, core, right, left, partner = place_of(group_size)
@@ -148,8 +148,14 @@
     def peer(turn, first, count, e):
         return remote(x_ref.at[e, 0:count], peer_hbm.at[e, pl.ds(first, count)], peer_s.at[turn, e], peer_r.at[turn, e], partner)
 
-    load_rows = pltpu.make_async_copy(hidden_hbm, rows.at[0, pl.ds(mine, tokens)], load_sem.at[0])
-    load_rows.start()
+    loads = (pltpu.make_async_copy(hidden_hbm, rows.at[0, pl.ds(mine, tokens)], load_sem.at[0]),
+             pltpu.make_async_copy(gain_hbm, gain_ref, load_sem.at[1]),
+             pltpu.make_async_copy(router_hbm, router_ref, load_sem.at[2]),
+             pltpu.make_async_copy(idx_hbm, idx_ref, load_sem.at[3]))
+    for copy in loads:
+        copy.start()
+    store_shared = pltpu.make_async_copy(shared_ref, shared_hbm, load_sem.at[4])
+    store_side = pltpu.make_async_copy(sides.at[0:group_size // CORES], side_hbm, load_sem.at[5])
 
     def normalise():
         block = 32
@@ -182,8 +188,8 @@
         for copy in gate_copies(slot, gate, up):
             copy.start()
 
-    def down_copy(down):
-        return pltpu.make_async_copy(down, down_buf, w_sem.at[4])
+    def down_copy(slot, down):
+        return pltpu.make_async_copy(down, down_buf.at[slot], w_sem.at[4 + slot])
 
     def shared_cols(ref, i):
         return ref.at[:, pl.ds(pl.multiple_of(i * ff, 128), ff)]
@@ -191,10 +197,12 @@
     neighbours = [device + cc for device in beside for cc in range(CORES)] + [partner]
     announce(neighbours)
     start_gate(0, shared_cols(sgate, 0), shared_cols(sup, 0))
-    down_copy(sdown.at[0:ff]).start()
+    down_copy(0, sdown.at[0:ff]).start()
     start_gate(1, shared_cols(sgate, 1), shared_cols(sup, 1))
+    down_copy(1, sdown.at[ff:2 * ff]).start()
     fill_before(before_ref)
-    load_rows.wait()
+    for copy in loads:
+        copy.wait()
     normalise()
     meet(neighbours)
     send(0)
@@ -214,8 +222,8 @@
         act = (jax.nn.silu(gate_out) * up_out).astype(BF16)
         next_gate()
         if fresh:
-            down_copy(wdown.at[0]).wait()
-        out = jnp.dot(act, down_buf[...], preferred_element_type=F32)
+            down_copy(slot, wdown.at[0]).wait()
+        out = jnp.dot(act, down_buf[slot], preferred_element_type=F32)
         next_down()
         return out
 
@@ -227,16 +235,8 @@
     def shared(i, carry):
         slot = i % 2
 
-        def next_down():
-            @pl.when(i == 0)
-            def _():
-                down_copy(sdown.at[ff:2 * ff]).start()
-
-            @pl.when(i == 1)
-            def _():
-                down_copy(wdown.at[0]).start()
         shared_ref[...] += swiglu(rows[0, pl.ds(mine, tokens), :], slot, True,
-                                  lambda: start_gate(slot, wgate.at[i], wup.at[i]), next_down)
+                                  lambda: start_gate(slot, wgate.at[i], wup.at[i]), lambda: down_copy(slot, wdown.at[i]).start())
         return carry
 
     shared_ref[...] = jnp.zeros_like(shared_ref)
@@ -270,8 +270,8 @@
         ahead = (e + 2) % local_count
         start_gate(slot, wgate.at[ahead], wup.at[ahead])
 
-    def down_after(e):
-        down_copy(wdown.at[(e + 1) % local_count]).start()
+    def down_after(e, slot):
+        down_copy(slot, wdown.at[(e + 2) % local_count]).start()
 
     def put(turn, first, count, e):
         stage_copy(e, first, count).start()
@@ -282,37 +282,36 @@
             @pl.when(e == local_count // 2)
             def _():
                 service(middle)
-            mlp(e, e % 2, 0, count, True, lambda: gate_after(e, e % 2), lambda: down_after(e))
+            mlp(e, e % 2, 0, count, True, lambda: gate_after(e, e % 2), lambda: down_after(e, e % 2))
             put(turn, first, count, e)
             return carry
         lax.fori_loop(0, local_count, one, 0)
 
     def last_experts(turn, first, count):
-        mlp(0, 0, 0, count - 1, True, nothing, nothing)
-        send_heads(1, 0)
+        def near(e, carry):
+            mlp(e, e % 2, 0, count - 1, True, nothing, nothing)
+            send_heads(1, e)
+            return carry
+
+        def far(e, carry):
+            mlp(e, e % 2, count - 1, 1, False, lambda: gate_after(e, e % 2), lambda: down_after(e, e % 2))
+            send_heads(0, e)
+            put(turn, first, count, e)
+            return carry
+
+        def both(e, carry):
+            mlp(e, e % 2, 0, count, True, nothing, nothing)
+            send_heads(1, e)
+            send_heads(0, e)
+            put(turn, first, count, e)
+            return carry
+
+        lax.fori_loop(0, 2, near, 0)
         service(6)
         partner_arrived(6)
         dispatch(first, first + count - 1, 1)
-        mlp(0, 0, count - 1, 1, False, lambda: gate_after(0, 0), lambda: down_after(0))
-        send_heads(0, 0)
-        put(turn, first, count, 0)
-
-        def one(e, carry):
-            def next_gate():
-                @pl.when(e < local_count - 2)
-                def _():
-                    gate_after(e, e % 2)
-
-            def next_down():
-                @pl.when(e < local_count - 1)
-                def _():
-                    down_after(e)
-            mlp(e, e % 2, 0, count, True, next_gate, next_down)
-            send_heads(1, e)
-            send_heads(0, e)
-            put(turn, first, count, e)
-            return carry
-        lax.fori_loop(1, local_count, one, 0)
+        lax.fori_loop(0, 2, far, 0)
+        lax.fori_loop(2, local_count, both, 0)
 
     def finish(turn, first, count):
         for e in range(local_count):
@@ -323,6 +322,7 @@
     own_part(other).wait_recv()
     own_tpart(1 - core).wait_recv()
     dispatch(0, 0, 1)
+    store_shared.start()
     service(1)
     partner_arrived(0)
     partner_arrived(1)
@@ -341,7 +341,7 @@
     dispatch(5, 5, 2)
     last_experts(2, 5, 3)
     finish(2, 5, 3)
-    side_out[...] = sides[0:group_size // CORES]
+    store_side.start()
     for way in range(2):
         for i in range(sends):
             ring(way, i).wait_send()
@@ -354,6 +354,8 @@
     for turn, (first, count) in enumerate(((0, 3), (3, 2), (5, 3))):
         for e in range(local_count):
             peer(turn, first, count, e).wait_recv()
+    store_shared.wait()
+    store_side.wait()
 
     def settle(e, carry):
         for step in range(2):
@@ -365,8 +367,8 @@
     lax.fori_loop(0, local_count, settle, 0)
 
 
-def scatter_kernel(group_size, capacity, rows_hbm, peer_hbm, head_hbm, side_ref, hidden_hbm, shared_hbm, out_ref,
-                   before_ref, hidden_ref, shared_ref, rows, heads, acc, ring_in, load_sem, head_sem, base_sem, ring_s, ring_r):
+def scatter_kernel(group_size, capacity, rows_hbm, peer_hbm, head_hbm, side_hbm, hidden_hbm, shared_hbm, out_ref,
+                   side_ref, before_ref, hidden_ref, shared_ref, rows, heads, acc, ring_in, load_sem, head_sem, base_sem, ring_s, ring_r):
     _, chip, core, right, left, _ = place_of(group_size)
     _, local_count, chips, _, hidden_size = rows.shape
     tokens = hidden_ref.shape[0]
@@ -384,6 +386,8 @@
 
     neighbours = (right, left)
     announce(neighbours)
+    load_side = pltpu.make_async_copy(side_hbm, side_ref, base_sem.at[2])
+    load_side.start()
     for i in range(2):
         for way in range(2):
             load_head(way, i).start()
@@ -435,6 +439,7 @@
             return carry
         lax.fori_loop(0, 2, one, 0)
 
+    load_side.wait()
     loaded = set()
 
     def ensure(ch):
@@ -500,14 +505,18 @@
         dma = pltpu.SemaphoreType.DMA
         expert_out, peer_out, heads, sides, shared_out = pl.pallas_call(
             functools.partial(gather_kernel, group_size, capacity, slots),
-            in_specs=[hbm, vmem, vmem, vmem] + [hbm] * 6,
-            out_specs=(hbm, hbm, hbm, vmem, vmem),
+            in_specs=[hbm] * 10,
+            out_specs=(hbm,) * 5,
             out_shape=(jax.ShapeDtypeStruct((local_count, chips, slots, hidden_size), BF16),
                        jax.ShapeDtypeStruct((local_count, chips, slots, hidden_size), BF16),
                        jax.ShapeDtypeStruct((2, 2, CORES, local_count, HEAD_ROWS, hidden_size // 2), BF16),
                        jax.ShapeDtypeStruct((chips, CORES, 16, tokens), F32),
                        jax.ShapeDtypeStruct((tokens, hidden_size), F32)),
             scratch_shapes=[
+                pltpu.VMEM((1, hidden_size), F32),
+                pltpu.VMEM((num_experts, hidden_size), BF16),
+                pltpu.VMEM((topk_idx.shape[1], tokens), jnp.int32),
+                pltpu.VMEM((tokens, hidden_size), F32),
                 pltpu.VMEM((tokens, tokens), BF16),
                 pltpu.VMEM((chips, CORES * tokens, hidden_size), BF16),
                 pltpu.VMEM((chips + 1, CORES, 16, tokens), F32),
@@ -515,22 +524,23 @@
                 pltpu.VMEM((local_count * slots, CORES * tokens), BF16),
                 pltpu.VMEM((2, hidden_size, ff), BF16),
                 pltpu.VMEM((2, hidden_size, ff), BF16),
-                pltpu.VMEM((ff, hidden_size), BF16),
+                pltpu.VMEM((2, ff, hidden_size), BF16),
                 dma((2, 7)), dma((2, 7)), dma((2, 7)), dma((2, 7)),
                 dma((2, 4)), dma((2, 4)), dma((2, 4)), dma((2, 4)),
                 dma((2,)), dma((2,)), dma((2, 2, local_count, CORES)), dma((2, 2, local_count, CORES)),
                 dma((3, local_count)), dma((3, local_count)),
-                dma((1,)), dma((5,)), dma((local_count,)),
+                dma((6,)), dma((6,)), dma((local_count,)),
             ],
             compiler_params=pltpu.CompilerParams(collective_id=0, has_side_effects=True, vmem_limit_bytes=VMEM_LIMIT),
             name='gather_experts',
         )(hidden, norm_gain[None, :], router_w.T, topk_idx.T, shared_gate, shared_up, shared_down, w_gate, w_up, w_down)
         return pl.pallas_call(
             functools.partial(scatter_kernel, group_size, capacity),
-            in_specs=[hbm, hbm, hbm, vmem, hbm, hbm],
+            in_specs=[hbm] * 6,
             out_specs=vmem,
             out_shape=jax.ShapeDtypeStruct((tokens, hidden_size), BF16),
             scratch_shapes=[
+                pltpu.VMEM((chips, CORES, 16, tokens), F32),
                 pltpu.VMEM((tokens, tokens), BF16),
                 pltpu.VMEM((tokens, hidden_size), BF16),
                 pltpu.VMEM((tokens, hidden_size), F32),
@@ -538,7 +548,7 @@
                 pltpu.VMEM((2, 2, CORES, local_count, WINDOW, hidden_size // 2), BF16),
                 pltpu.VMEM((2, 2, tokens, hidden_size // 2), F32),
                 pltpu.VMEM((2, 5, tokens, hidden_size // 2), F32),
-                dma((CORES, chips)), dma((2, 2)), dma((2,)), dma((2, 5)), dma((2, 5)),
+                dma((CORES, chips)), dma((2, 2)), dma((3,)), dma((2, 5)), dma((2, 5)),
             ],
             compiler_params=pltpu.CompilerParams(collective_id=1, has_side_effects=True, vmem_limit_bytes=VMEM_LIMIT),
             name='combine_scatter',

time: 262 us -> 253 us (0.966)
  Pallas kernels: 259 us -> 251 us
    pallas_call x1, Pallas kernels: 135 us -> 127 us  [local_step(): pl.pallas_call(functools.partial(gather_kernel, group_size, capacity, slo...]
where the time goes in v3:
time: 253 us
  Pallas kernels  251 us (99%)
    pallas_call x1, Pallas kernels, local_step(): pl.pallas_call(functools.partial(gather_kernel, group_size, capacity, slo...  127 us
    pallas_call x1, Pallas kernels, local_step(): pl.pallas_call(functools.partial(scatter_kernel, group_size, capacity), i...  124 us

profile of v3, /device:TPU:21, one launch (start us, length us, event | category | flops | bytes accessed | tf_op | source)
XLA Modules:
  0.0 253.2 jit_solution(10182953924327458367)
XLA Ops:
  0.0 126.7 %gather_experts.1 = (bf16[4,8,80,2048]{3,2,1,0:T(8,128)(2,1)}, bf16[4,8,80,2048]{3,2,1,0:T(8,128)(2,1)}, bf16[2,2,2,4,40,1024]{5,4,3,2,1,0:T(8,128)(2,1)}, f32[8,2,16,256]{3,2,1,0:T(8,128)}, f32[256,2048]{1,0:T(8,128)}) custom-call(bf16[256,2048]{1,0:T(8,128)(2,1)} %hidden_hbm.3, f32[1,2048]{1,0:T(1,128)} %bitcast.4, bf16[64,2048]{1,0:T(8,128)(2,1)} %bitcast.3, ...), custom_call_target="tpu_custom_call" | custom-call | tf_op jit(solution)/shard_map/gather_experts/pallas_call | solution.py:506
  126.8 124.1 %combine_scatter.1 = bf16[256,2048]{1,0:T(8,128)(2,1)} custom-call(bf16[4,8,80,2048]{3,2,1,0:T(8,128)(2,1)} %get-tuple-element.10.rows_hbm, bf16[4,8,80,2048]{3,2,1,0:T(8,128)(2,1)} %get-tuple-element.11.peer_hbm, bf16[2,2,2,4,40,1024]{5,4,3,2,1,0:T(8,128)(2,1)} %get-tuple-element.12.head_hbm, f32[8,2,16,256]{3,2,1,0:T(8,128)} %get-tuple-element.13.side_hbm, ...), custom_call_target="tpu_custom_call" | custom-call | tf_op jit(solution)/shard_map/combine_scatter/pallas_call | solution.py:537
  250.9 2.3 copy.12

commit v4 on v3

--- a/solution.py
+++ b/solution.py
@@ -196,13 +196,13 @@
 
     neighbours = [device + cc for device in beside for cc in range(CORES)] + [partner]
     announce(neighbours)
+    fill_before(before_ref)
+    for copy in loads:
+        copy.wait()
     start_gate(0, shared_cols(sgate, 0), shared_cols(sup, 0))
     down_copy(0, sdown.at[0:ff]).start()
     start_gate(1, shared_cols(sgate, 1), shared_cols(sup, 1))
     down_copy(1, sdown.at[ff:2 * ff]).start()
-    fill_before(before_ref)
-    for copy in loads:
-        copy.wait()
     normalise()
     meet(neighbours)
     send(0)
@@ -388,18 +388,15 @@
     announce(neighbours)
     load_side = pltpu.make_async_copy(side_hbm, side_ref, base_sem.at[2])
     load_side.start()
-    for i in range(2):
+    def start_loads(i):
         for way in range(2):
             load_head(way, i).start()
             for copy in load((last - 1, last - 2, 4, 3)[2 * i + way]):
                 copy.start()
-    for ch in (2, 1, 0):
-        for copy in load(ch):
-            copy.start()
+
     load_base = (pltpu.make_async_copy(hidden_hbm, hidden_ref, base_sem.at[0]),
                  pltpu.make_async_copy(shared_hbm, shared_ref, base_sem.at[1]))
-    for copy in load_base:
-        copy.start()
+    start_loads(0)
     fill_before(before_ref)
     heads[:, :, :, :, HEAD_ROWS:WINDOW, :] = jnp.zeros((2, 2, CORES, local_count, WINDOW - HEAD_ROWS, half), BF16)
 
@@ -458,6 +455,13 @@
                 load_head(way, i).wait()
             else:
                 ring(way, i - 2).wait_send()
+        if i == 0:
+            start_loads(1)
+            for ch in (2, 1, 0):
+                for copy in load(ch):
+                    copy.start()
+            for copy in load_base:
+                copy.start()
         units(i, chans, (i % 2, 1 - i % 2))
         if i == 0:
             meet(neighbours)
@@ -538,7 +542,7 @@
             functools.partial(scatter_kernel, group_size, capacity),
             in_specs=[hbm] * 6,
             out_specs=vmem,
-            out_shape=jax.ShapeDtypeStruct((tokens, hidden_size), BF16),
+            out_shape=pltpu.VMEM((tokens, hidden_size), BF16),
             scratch_shapes=[
                 pltpu.VMEM((chips, CORES, 16, tokens), F32),
                 pltpu.VMEM((tokens, tokens), BF16),
@@ -550,7 +554,8 @@
                 pltpu.VMEM((2, 5, tokens, hidden_size // 2), F32),
                 dma((CORES, chips)), dma((2, 2)), dma((3,)), dma((2, 5)), dma((2, 5)),
             ],
-            compiler_params=pltpu.CompilerParams(collective_id=1, has_side_effects=True, vmem_limit_bytes=VMEM_LIMIT),
+            compiler_params=pltpu.CompilerParams(collective_id=1, has_side_effects=True,
+                                                 vmem_limit_bytes=VMEM_LIMIT - 2 * tokens * hidden_size - 65536),
             name='combine_scatter',
         )(expert_out, peer_out, heads, sides, hidden, shared_out)
 

time: 253 us -> 249 us (0.984)
  Pallas kernels: 251 us -> 248 us
    pallas_call x1, Pallas kernels: 124 us -> 122 us  [local_step(): pl.pallas_call(functools.partial(scatter_kernel, group_size, capacity), i...]
where the time goes in v4:
time: 249 us
  Pallas kernels  248 us (100%)
    pallas_call x1, Pallas kernels, local_step(): pl.pallas_call(functools.partial(gather_kernel, group_size, capacity, slo...  127 us
    pallas_call x1, Pallas kernels, local_step(): pl.pallas_call(functools.partial(scatter_kernel, group_size, capacity), i...  122 us

profile of v4, /device:TPU:21, one launch (start us, length us, event | category | flops | bytes accessed | tf_op | source)
XLA Modules:
  0.0 249.2 jit_solution(7615504929334389343)
XLA Ops:
  0.0 126.7 %gather_experts.1 = (bf16[4,8,80,2048]{3,2,1,0:T(8,128)(2,1)}, bf16[4,8,80,2048]{3,2,1,0:T(8,128)(2,1)}, bf16[2,2,2,4,40,1024]{5,4,3,2,1,0:T(8,128)(2,1)}, f32[8,2,16,256]{3,2,1,0:T(8,128)}, f32[256,2048]{1,0:T(8,128)}) custom-call(bf16[256,2048]{1,0:T(8,128)(2,1)} %hidden_hbm.3, f32[1,2048]{1,0:T(1,128)} %bitcast.4, bf16[64,2048]{1,0:T(8,128)(2,1)} %bitcast.3, ...), custom_call_target="tpu_custom_call" | custom-call | tf_op jit(solution)/shard_map/gather_experts/pallas_call | solution.py:510
  126.8 121.5 %combine_scatter.1 = bf16[256,2048]{1,0:T(8,128)(2,1)S(1)} custom-call(bf16[4,8,80,2048]{3,2,1,0:T(8,128)(2,1)} %get-tuple-element.10.rows_hbm, bf16[4,8,80,2048]{3,2,1,0:T(8,128)(2,1)} %get-tuple-element.11.peer_hbm, bf16[2,2,2,4,40,1024]{5,4,3,2,1,0:T(8,128)(2,1)} %get-tuple-element.12.head_hbm, f32[8,2,16,256]{3,2,1,0:T(8,128)} %get-tuple-element.13.side_hbm, ...), custom_call_target="tpu_custom_call" | custom-call | tf_op jit(solution)/shard_map/combine_scatter/pallas_call | solution.py:541
  248.3 1.0 copy.12

commit v5 on v4

--- a/solution.py
+++ b/solution.py
@@ -157,16 +157,16 @@
     store_shared = pltpu.make_async_copy(shared_ref, shared_hbm, load_sem.at[4])
     store_side = pltpu.make_async_copy(sides.at[0:group_size // CORES], side_hbm, load_sem.at[5])
 
-    def normalise():
+    def normalise(r):
         block = 32
 
         def one(i, carry):
-            place = pl.ds(pl.multiple_of(mine + i * block, block), block)
+            place = pl.ds(pl.multiple_of(mine + r * half + i * block, block), block)
             x = rows[0, place, :].astype(F32)
             inv_rms = lax.rsqrt(jnp.mean(x * x, axis=-1, keepdims=True) + NORM_EPS)
             rows[0, place, :] = (x * inv_rms * gain_ref[...]).astype(BF16)
             return carry
-        lax.fori_loop(0, tokens // block, one, 0)
+        lax.fori_loop(0, half // block, one, 0)
 
     def route():
         x = rows[0, pl.ds(mine, tokens), :]
@@ -203,9 +203,11 @@
     down_copy(0, sdown.at[0:ff]).start()
     start_gate(1, shared_cols(sgate, 1), shared_cols(sup, 1))
     down_copy(1, sdown.at[ff:2 * ff]).start()
-    normalise()
+    normalise(0)
     meet(neighbours)
-    send(0)
+    ring(0, 0).start()
+    normalise(1)
+    ring(1, 0).start()
     send(1)
     own_part(mine).start()
     route()
@@ -328,14 +330,14 @@
     partner_arrived(1)
     dispatch(0, 1, 2)
     experts(0, 0, 3, 2)
+    service(3)
     finish(0, 0, 3)
-    service(3)
     partner_arrived(2)
     partner_arrived(3)
     dispatch(3, 3, 2)
     experts(1, 3, 2, 4)
+    service(5)
     finish(1, 3, 2)
-    service(5)
     partner_arrived(4)
     partner_arrived(5)
     dispatch(5, 5, 2)

time: 249 us -> 249 us (level)
  no operation moved by 1% of the time
where the time goes in v5:
time: 249 us
  Pallas kernels  248 us (100%)
    pallas_call x1, Pallas kernels, local_step(): pl.pallas_call(functools.partial(gather_kernel, group_size, capacity, slo...  126 us
    pallas_call x1, Pallas kernels, local_step(): pl.pallas_call(functools.partial(scatter_kernel, group_size, capacity), i...  122 us

profile of v5, /device:TPU:21, one launch (start us, length us, event | category | flops | bytes accessed | tf_op | source)
XLA Modules:
  0.0 249.4 jit_solution(1470994075233777654)
XLA Ops:
  0.0 126.0 %gather_experts.1 = (bf16[4,8,80,2048]{3,2,1,0:T(8,128)(2,1)}, bf16[4,8,80,2048]{3,2,1,0:T(8,128)(2,1)}, bf16[2,2,2,4,40,1024]{5,4,3,2,1,0:T(8,128)(2,1)}, f32[8,2,16,256]{3,2,1,0:T(8,128)}, f32[256,2048]{1,0:T(8,128)}) custom-call(bf16[256,2048]{1,0:T(8,128)(2,1)} %hidden_hbm.3, f32[1,2048]{1,0:T(1,128)} %bitcast.4, bf16[64,2048]{1,0:T(8,128)(2,1)} %bitcast.3, ...), custom_call_target="tpu_custom_call" | custom-call | tf_op jit(solution)/shard_map/gather_experts/pallas_call | solution.py:512
  126.0 122.4 %combine_scatter.1 = bf16[256,2048]{1,0:T(8,128)(2,1)S(1)} custom-call(bf16[4,8,80,2048]{3,2,1,0:T(8,128)(2,1)} %get-tuple-element.10.rows_hbm, bf16[4,8,80,2048]{3,2,1,0:T(8,128)(2,1)} %get-tuple-element.11.peer_hbm, bf16[2,2,2,4,40,1024]{5,4,3,2,1,0:T(8,128)(2,1)} %get-tuple-element.12.head_hbm, f32[8,2,16,256]{3,2,1,0:T(8,128)} %get-tuple-element.13.side_hbm, ...), custom_call_target="tpu_custom_call" | custom-call | tf_op jit(solution)/shard_map/combine_scatter/pallas_call | solution.py:543
  248.4 1.0 copy.12
